TPU v7x, 32 devices: a whole 2x2x4 slice. The times are simulated.
32 devices in a mesh: asset: 8 (over y, x, core), tm: 4 (over z).
Axes of the slice: x: 2, y: 2, z: 4, core: 2. Of those that a mesh axis runs over, the one named last changes fastest.
Arguments:
- day_ranks: int32 [144, 4096], P('tm', 'asset'), may hold values from 2 to 240
- confidence: float32 [144, 4096], P('tm', 'asset'), may hold values from 0.25 to 4
Outputs:
- correlation: bfloat16 [24, 4096, 4096], P('tm', 'asset')
All inputs are finite; a program needn't handle non-finite values.
Results may differ from a plain program's by a relative error of at most 0.001.
Values sent between devices are 32-bit elements; how exact they have to be, the bound alone decides.
No kernel may reach another device: no remote copies, remote signals or barrier semaphores. Data moves between devices by JAX's collectives and lax.ppermute only.
A program may use at most 64 MiB of HBM per device.

v0:
```python
import jax
import jax.numpy as jnp
from jax import lax
from jax.sharding import PartitionSpec as P

WIN = 120
ENDS_DEV = 6
SPAN = 125


epsilon = 1e-06


def shifted(value, axis, steps):
    count = lax.axis_size(axis)
    pairs = [(source, (source + steps) % count) for source in range(count)]
    return lax.ppermute(value, axis, pairs)


def window_moments(span_rows):
    windows = jnp.stack([span_rows[offset : offset + WIN] for offset in range(ENDS_DEV)])
    window_mean = jnp.sum(windows, 1) / WIN
    centred = windows - window_mean[:, None, :]
    window_scale = lax.rsqrt(jnp.sum(centred * centred, 1) / WIN + epsilon)
    return (window_mean, window_scale)


def window_gram(left_rows, right_rows, start_index, stop_index):
    return lax.dot_general(
        left_rows[start_index:stop_index],
        right_rows[start_index:stop_index],
        (((0,), (0,)), ((), ())),
        precision=lax.Precision.HIGHEST,
        preferred_element_type=jnp.float32,
    )


def cross_tile(own_span, own_moments, other_span):
    other_mean, other_scale = window_moments(other_span)
    own_mean, own_scale = own_moments
    gram_sums = jnp.stack(
        [window_gram(own_span, other_span, offset, offset + WIN) for offset in range(ENDS_DEV)]
    )
    centre = own_mean[:, :, None] * other_mean[:, None, :]
    spread = own_scale[:, :, None] * other_scale[:, None, :]
    return ((gram_sums / WIN - centre) * spread).astype(jnp.bfloat16)


def per_device(day_ranks, confidence):
    days_dev = day_ranks.shape[0]
    block_width = day_ranks.shape[1]
    time_count = lax.axis_size("tm")
    asset_count = lax.axis_size("asset")
    lead_days = days_dev * time_count - ENDS_DEV * time_count - WIN + 1
    scores = confidence * (day_ranks - (WIN + 1)).astype(jnp.float32) / WIN
    all_days = lax.all_gather(scores, "tm", axis=0, tiled=True)
    first_day = lead_days + lax.axis_index("tm") * ENDS_DEV
    own_span = lax.dynamic_slice_in_dim(all_days, first_day, SPAN, 0)
    own_moments = window_moments(own_span)
    own_index = lax.axis_index("asset")
    output = jnp.zeros((ENDS_DEV, block_width, block_width * asset_count), jnp.bfloat16)
    output = lax.dynamic_update_slice_in_dim(
        output, cross_tile(own_span, own_moments, own_span), own_index * block_width, 2
    )

    def rotate_once(step_count, loop_state):
        current, visitor = loop_state
        visitor = shifted(visitor, "asset", 1)
        source_index = (own_index - step_count) % asset_count
        current = lax.dynamic_update_slice_in_dim(
            current, cross_tile(own_span, own_moments, visitor), source_index * block_width, 2
        )
        return (current, visitor)

    output, visitor = lax.fori_loop(1, asset_count, rotate_once, (output, own_span))
    return output


def solution(mesh):
    return jax.shard_map(
        per_device,
        mesh=mesh,
        in_specs=(P("tm", "asset"), P("tm", "asset")),
        out_specs=P("tm", "asset", None),
        check_vma=False,
    )
```

profile of v0, /device:TPU:0, one launch (start us, length us, event | category | flops | bytes accessed | tf_op | source)
XLA Modules:
  0.0 150.2 jit_solution(6611642929315742618)
XLA Ops:
  0.9 15.9 %all-gather = f32[4,36,512]{2,1,0:T(8,128)S(1)} all-gather(f32[1,36,512]{2,1,0:T(8,128)S(1)} %multiply_bitcast_fusion), channel_id=1, replica_groups=mesh['asset'=8,'tm'=4] {'tm'}, dimensions={0}, use_global_device_ids=true | all-gather | bytes 368640 | tf_op jit(solution)/shard_map/all_gather | solution.py:56
  17.6 1.0 fusion.25
  18.6 1.0 fusion.24
  19.7 1.0 fusion.23
  20.7 1.0 fusion.22
  21.7 1.0 fusion.21
  22.8 1.0 fusion.20
  23.8 3.1 %broadcast_in_dim.10 = bf16[6,512,4096]{2,1,0:T(8,128)(2,1)S(1)} broadcast(bf16[]{:T(256)} %constant.126.clone.1), dimensions={} | broadcast | bytes 25165826 | tf_op jit(solution)/shard_map/broadcast_in_dim | solution.py:61
  26.9 1.4 fusion.19
  28.3 8.9 %copy-done = bf16[6,512,4096]{2,1,0:T(8,128)(2,1)} copy-done((bf16[6,512,4096]{2,1,0:T(8,128)(2,1)}, bf16[6,512,4096]{2,1,0:T(8,128)(2,1)S(1)}, u32[]{:S(2)}) %copy-start) | copy-done | bytes 25165848
  37.2 112.8 %while.17 = (s32[]{:T(128)}, bf16[6,512,4096]{2,1,0:T(8,128)(2,1)}, f32[125,512]{1,0:T(8,128)S(1)}, f32[125,512]{1,0:T(8,128)S(1)}, f32[6,512]{1,0:T(8,128)S(1)}...) while((s32[]{:T(128)}, bf16[6,512,4096]{2,1,0:T(8,128)(2,1)}, ...), condition=%wide.region_5.6_spmd, body=%wide.region_2.5_spmd.sunk | while | flops 2275838976 | bytes 26247516 | solution.py:75
  37.2 6.7 %collective-permute-done = f32[125,512]{1,0:T(8,128)S(1)} collective-permute-done((f32[125,512]{1,0:T(8,128)S(1)}, f32[125,512]{1,0:T(8,128)S(1)}, u32[]{:S(2)}, u32[]{:S(2)}) %collective-permute-start) | collective-permute-done | bytes 256032 | tf_op jit(solution)/shard_map/while/body/eval_jaxpr/ppermute | solution.py:17
  44.5 1.0 fusion.69
  48.7 1.0 fusion.73
  49.7 1.0 fusion.74
  50.8 2.5 %fusion.75 = bf16[6,512,4096]{2,1,0:T(8,128)(2,1)} fusion(bf16[6,512,4096]{2,1,0:T(8,128)(2,1)} %get-tuple-element.255, s32[]{:T(128)S(6)} %select_n.41, f32[6,512,512]{2,1,0:T(8,128)S(1)} %fusion.74, f32[6,512]{1,0:T(8,128)S(1)} %add_rsqrt_fusion.3, f32[6,512]{1,0:T(8,128)S(1)} %get-tuple-element.273, f32[6,512]{1,0:T(8,128)S(1)} %broadcast_multiply_fusion.3, ...), kind=kLoop, calls=%fused_computation.1.clone.1 | loop fusion | flops 9437184 | bytes 9486340 | tf_op jit(solution)/shard_map/while/body/eval_jaxpr/dynamic_update_slice | solution.py:70
  53.4 6.7 %collective-permute-done = f32[125,512]{1,0:T(8,128)S(1)} collective-permute-done((f32[125,512]{1,0:T(8,128)S(1)}, f32[125,512]{1,0:T(8,128)S(1)}, u32[]{:S(2)}, u32[]{:S(2)}) %collective-permute-start) | collective-permute-done | bytes 256032 | tf_op jit(solution)/shard_map/while/body/eval_jaxpr/ppermute | solution.py:17
  60.6 1.0 fusion.69
  61.7 1.0 fusion.70
  62.7 1.0 fusion.71
  64.8 1.0 fusion.73
  66.9 2.5 %fusion.75 = bf16[6,512,4096]{2,1,0:T(8,128)(2,1)} fusion(bf16[6,512,4096]{2,1,0:T(8,128)(2,1)} %get-tuple-element.255, s32[]{:T(128)S(6)} %select_n.41, f32[6,512,512]{2,1,0:T(8,128)S(1)} %fusion.74, f32[6,512]{1,0:T(8,128)S(1)} %add_rsqrt_fusion.3, f32[6,512]{1,0:T(8,128)S(1)} %get-tuple-element.273, f32[6,512]{1,0:T(8,128)S(1)} %broadcast_multiply_fusion.3, ...), kind=kLoop, calls=%fused_computation.1.clone.1 | loop fusion | flops 9437184 | bytes 9486340 | tf_op jit(solution)/shard_map/while/body/eval_jaxpr/dynamic_update_slice | solution.py:70
  69.5 6.7 %collective-permute-done = f32[125,512]{1,0:T(8,128)S(1)} collective-permute-done((f32[125,512]{1,0:T(8,128)S(1)}, f32[125,512]{1,0:T(8,128)S(1)}, u32[]{:S(2)}, u32[]{:S(2)}) %collective-permute-start) | collective-permute-done | bytes 256032 | tf_op jit(solution)/shard_map/while/body/eval_jaxpr/ppermute | solution.py:17
  76.8 1.0 fusion.69
  79.9 1.0 fusion.72
  82.0 1.0 fusion.74
  83.0 2.5 %fusion.75 = bf16[6,512,4096]{2,1,0:T(8,128)(2,1)} fusion(bf16[6,512,4096]{2,1,0:T(8,128)(2,1)} %get-tuple-element.255, s32[]{:T(128)S(6)} %select_n.41, f32[6,512,512]{2,1,0:T(8,128)S(1)} %fusion.74, f32[6,512]{1,0:T(8,128)S(1)} %add_rsqrt_fusion.3, f32[6,512]{1,0:T(8,128)S(1)} %get-tuple-element.273, f32[6,512]{1,0:T(8,128)S(1)} %broadcast_multiply_fusion.3, ...), kind=kLoop, calls=%fused_computation.1.clone.1 | loop fusion | flops 9437184 | bytes 9486340 | tf_op jit(solution)/shard_map/while/body/eval_jaxpr/dynamic_update_slice | solution.py:70
  85.7 6.7 %collective-permute-done = f32[125,512]{1,0:T(8,128)S(1)} collective-permute-done((f32[125,512]{1,0:T(8,128)S(1)}, f32[125,512]{1,0:T(8,128)S(1)}, u32[]{:S(2)}, u32[]{:S(2)}) %collective-permute-start) | collective-permute-done | bytes 256032 | tf_op jit(solution)/shard_map/while/body/eval_jaxpr/ppermute | solution.py:17
  92.9 1.0 fusion.69
  93.9 1.0 fusion.70
  95.0 1.0 fusion.71
  97.1 1.0 fusion.73
  99.1 2.5 %fusion.75 = bf16[6,512,4096]{2,1,0:T(8,128)(2,1)} fusion(bf16[6,512,4096]{2,1,0:T(8,128)(2,1)} %get-tuple-element.255, s32[]{:T(128)S(6)} %select_n.41, f32[6,512,512]{2,1,0:T(8,128)S(1)} %fusion.74, f32[6,512]{1,0:T(8,128)S(1)} %add_rsqrt_fusion.3, f32[6,512]{1,0:T(8,128)S(1)} %get-tuple-element.273, f32[6,512]{1,0:T(8,128)S(1)} %broadcast_multiply_fusion.3, ...), kind=kLoop, calls=%fused_computation.1.clone.1 | loop fusion | flops 9437184 | bytes 9486340 | tf_op jit(solution)/shard_map/while/body/eval_jaxpr/dynamic_update_slice | solution.py:70
  101.8 6.7 %collective-permute-done = f32[125,512]{1,0:T(8,128)S(1)} collective-permute-done((f32[125,512]{1,0:T(8,128)S(1)}, f32[125,512]{1,0:T(8,128)S(1)}, u32[]{:S(2)}, u32[]{:S(2)}) %collective-permute-start) | collective-permute-done | bytes 256032 | tf_op jit(solution)/shard_map/while/body/eval_jaxpr/ppermute | solution.py:17
  109.0 1.0 fusion.69
  112.1 1.0 fusion.72
  114.2 1.0 fusion.74
  115.3 2.5 %fusion.75 = bf16[6,512,4096]{2,1,0:T(8,128)(2,1)} fusion(bf16[6,512,4096]{2,1,0:T(8,128)(2,1)} %get-tuple-element.255, s32[]{:T(128)S(6)} %select_n.41, f32[6,512,512]{2,1,0:T(8,128)S(1)} %fusion.74, f32[6,512]{1,0:T(8,128)S(1)} %add_rsqrt_fusion.3, f32[6,512]{1,0:T(8,128)S(1)} %get-tuple-element.273, f32[6,512]{1,0:T(8,128)S(1)} %broadcast_multiply_fusion.3, ...), kind=kLoop, calls=%fused_computation.1.clone.1 | loop fusion | flops 9437184 | bytes 9486340 | tf_op jit(solution)/shard_map/while/body/eval_jaxpr/dynamic_update_slice | solution.py:70
  117.9 6.7 %collective-permute-done = f32[125,512]{1,0:T(8,128)S(1)} collective-permute-done((f32[125,512]{1,0:T(8,128)S(1)}, f32[125,512]{1,0:T(8,128)S(1)}, u32[]{:S(2)}, u32[]{:S(2)}) %collective-permute-start) | collective-permute-done | bytes 256032 | tf_op jit(solution)/shard_map/while/body/eval_jaxpr/ppermute | solution.py:17
  125.1 1.0 fusion.69
  126.2 1.0 fusion.70
  127.2 1.0 fusion.71
  129.3 1.0 fusion.73
  131.4 2.5 %fusion.75 = bf16[6,512,4096]{2,1,0:T(8,128)(2,1)} fusion(bf16[6,512,4096]{2,1,0:T(8,128)(2,1)} %get-tuple-element.255, s32[]{:T(128)S(6)} %select_n.41, f32[6,512,512]{2,1,0:T(8,128)S(1)} %fusion.74, f32[6,512]{1,0:T(8,128)S(1)} %add_rsqrt_fusion.3, f32[6,512]{1,0:T(8,128)S(1)} %get-tuple-element.273, f32[6,512]{1,0:T(8,128)S(1)} %broadcast_multiply_fusion.3, ...), kind=kLoop, calls=%fused_computation.1.clone.1 | loop fusion | flops 9437184 | bytes 9486340 | tf_op jit(solution)/shard_map/while/body/eval_jaxpr/dynamic_update_slice | solution.py:70
  134.0 6.7 %collective-permute-done = f32[125,512]{1,0:T(8,128)S(1)} collective-permute-done((f32[125,512]{1,0:T(8,128)S(1)}, f32[125,512]{1,0:T(8,128)S(1)}, u32[]{:S(2)}, u32[]{:S(2)}) %collective-permute-start) | collective-permute-done | bytes 256032 | tf_op jit(solution)/shard_map/while/body/eval_jaxpr/ppermute | solution.py:17
  141.3 1.0 fusion.69
  144.4 1.0 fusion.72
  147.5 2.5 %fusion.75 = bf16[6,512,4096]{2,1,0:T(8,128)(2,1)} fusion(bf16[6,512,4096]{2,1,0:T(8,128)(2,1)} %get-tuple-element.255, s32[]{:T(128)S(6)} %select_n.41, f32[6,512,512]{2,1,0:T(8,128)S(1)} %fusion.74, f32[6,512]{1,0:T(8,128)S(1)} %add_rsqrt_fusion.3, f32[6,512]{1,0:T(8,128)S(1)} %get-tuple-element.273, f32[6,512]{1,0:T(8,128)S(1)} %broadcast_multiply_fusion.3, ...), kind=kLoop, calls=%fused_computation.1.clone.1 | loop fusion | flops 9437184 | bytes 9486340 | tf_op jit(solution)/shard_map/while/body/eval_jaxpr/dynamic_update_slice | solution.py:70
  (118 shorter events, 25.2 us)
Async XLA Ops:
  28.3 8.9 %copy-start = (bf16[6,512,4096]{2,1,0:T(8,128)(2,1)}, bf16[6,512,4096]{2,1,0:T(8,128)(2,1)S(1)}, u32[]{:S(2)}) copy-start(bf16[6,512,4096]{2,1,0:T(8,128)(2,1)S(1)} %fusion.19) | copy-start | bytes 75497472
  37.2 6.7 %collective-permute-start = (f32[125,512]{1,0:T(8,128)S(1)}, f32[125,512]{1,0:T(8,128)S(1)}, u32[]{:S(2)}, u32[]{:S(2)}) collective-permute-start(f32[125,512]{1,0:T(8,128)S(1)} %get-tuple-element.256), channel_id=1, source_target_pairs={{0,4},{4,8},{8,12},{12,16},{16,20},{20,24},{24,28},{28,0},{1,5},{5... | collective-permute-start | bytes 768008 | tf_op jit(solution)/shard_map/while/body/eval_jaxpr/ppermute | solution.py:17
  53.3 6.7 %collective-permute-start = (f32[125,512]{1,0:T(8,128)S(1)}, f32[125,512]{1,0:T(8,128)S(1)}, u32[]{:S(2)}, u32[]{:S(2)}) collective-permute-start(f32[125,512]{1,0:T(8,128)S(1)} %get-tuple-element.256), channel_id=1, source_target_pairs={{0,4},{4,8},{8,12},{12,16},{16,20},{20,24},{24,28},{28,0},{1,5},{5... | collective-permute-start | bytes 768008 | tf_op jit(solution)/shard_map/while/body/eval_jaxpr/ppermute | solution.py:17
  69.4 6.7 %collective-permute-start = (f32[125,512]{1,0:T(8,128)S(1)}, f32[125,512]{1,0:T(8,128)S(1)}, u32[]{:S(2)}, u32[]{:S(2)}) collective-permute-start(f32[125,512]{1,0:T(8,128)S(1)} %get-tuple-element.256), channel_id=1, source_target_pairs={{0,4},{4,8},{8,12},{12,16},{16,20},{20,24},{24,28},{28,0},{1,5},{5... | collective-permute-start | bytes 768008 | tf_op jit(solution)/shard_map/while/body/eval_jaxpr/ppermute | solution.py:17
  85.6 6.7 %collective-permute-start = (f32[125,512]{1,0:T(8,128)S(1)}, f32[125,512]{1,0:T(8,128)S(1)}, u32[]{:S(2)}, u32[]{:S(2)}) collective-permute-start(f32[125,512]{1,0:T(8,128)S(1)} %get-tuple-element.256), channel_id=1, source_target_pairs={{0,4},{4,8},{8,12},{12,16},{16,20},{20,24},{24,28},{28,0},{1,5},{5... | collective-permute-start | bytes 768008 | tf_op jit(solution)/shard_map/while/body/eval_jaxpr/ppermute | solution.py:17
  101.7 6.7 %collective-permute-start = (f32[125,512]{1,0:T(8,128)S(1)}, f32[125,512]{1,0:T(8,128)S(1)}, u32[]{:S(2)}, u32[]{:S(2)}) collective-permute-start(f32[125,512]{1,0:T(8,128)S(1)} %get-tuple-element.256), channel_id=1, source_target_pairs={{0,4},{4,8},{8,12},{12,16},{16,20},{20,24},{24,28},{28,0},{1,5},{5... | collective-permute-start | bytes 768008 | tf_op jit(solution)/shard_map/while/body/eval_jaxpr/ppermute | solution.py:17
  117.8 6.7 %collective-permute-start = (f32[125,512]{1,0:T(8,128)S(1)}, f32[125,512]{1,0:T(8,128)S(1)}, u32[]{:S(2)}, u32[]{:S(2)}) collective-permute-start(f32[125,512]{1,0:T(8,128)S(1)} %get-tuple-element.256), channel_id=1, source_target_pairs={{0,4},{4,8},{8,12},{12,16},{16,20},{20,24},{24,28},{28,0},{1,5},{5... | collective-permute-start | bytes 768008 | tf_op jit(solution)/shard_map/while/body/eval_jaxpr/ppermute | solution.py:17
  133.9 6.7 %collective-permute-start = (f32[125,512]{1,0:T(8,128)S(1)}, f32[125,512]{1,0:T(8,128)S(1)}, u32[]{:S(2)}, u32[]{:S(2)}) collective-permute-start(f32[125,512]{1,0:T(8,128)S(1)} %get-tuple-element.256), channel_id=1, source_target_pairs={{0,4},{4,8},{8,12},{12,16},{16,20},{20,24},{24,28},{28,0},{1,5},{5... | collective-permute-start | bytes 768008 | tf_op jit(solution)/shard_map/while/body/eval_jaxpr/ppermute | solution.py:17
where the time goes:
time: 150 us
  matrix products  49.6 us (33%)
  waiting for transfers between devices  46.6 us (31%)
  other arithmetic  23 us (15%)
  blocking collectives  15.9 us (11%)
  local copies, waits for them, and re-layouts  13.3 us (9%)
    dot_general x48, matrix products, window_gram(): lax.dot_general(left_rows[start_index:stop_index], right_rows[start_index...  49.6 us
    ppermute x7, waiting for transfers between devices, shifted(): return lax.ppermute(value, axis, pairs)  46.6 us
    dynamic_update_slice x7, other arithmetic, rotate_once(): lax.dynamic_update_slice_in_dim(current, cross_tile(own_span, own_moments...  17.7 us
    all_gather x1, blocking collectives, per_device(): all_days = lax.all_gather(scores, 'tm', axis=0, tiled=True)  15.9 us
    unnamed x9, local copies, waits for them, and re-layouts  9.12 us
    broadcast_in_dim x1, local copies, waits for them, and re-layouts, per_device(): jnp.zeros((ENDS_DEV, block_width, block_width * asset_count), jnp.bfloat16)  3.06 us
  transfers between devices with their start and end apart: 7, of which 7 were waited for; matrix products, arithmetic and copies ran while one was open for 0% of the time, Pallas kernels for 0%

commit v1 on v0

v1 whole, which is shorter than its diff:
```python
import jax
import jax.numpy as jnp
from jax import lax
from jax.experimental import pallas as pl
from jax.experimental.pallas import tpu as pltpu
from jax.sharding import PartitionSpec as P


WIN = 120
ENDS_DEV = 6
ROWS = 128
EDGE = 16


epsilon = 1e-06


def window_stats(span, offset):
    rows, width = span.shape
    inner = rows - 2 * EDGE
    centre = jnp.sum(span[EDGE : rows - EDGE], 0, keepdims=True) * (1.0 / inner)
    shifted = span - centre
    middle = shifted[EDGE : rows - EDGE]
    middle_sum = jnp.sum(middle, 0, keepdims=True)
    middle_square = jnp.sum(middle * middle, 0, keepdims=True)
    edge = jnp.concatenate([shifted[:EDGE], shifted[rows - EDGE :]], 0)
    edge_square = edge * edge
    row = lax.broadcasted_iota(jnp.int32, (2 * EDGE, width), 0)
    day = jnp.where(row < EDGE, row, row + inner) - offset
    means, scales = [], []
    for end in range(ENDS_DEV):
        inside = (day >= end) & (day < end + WIN)
        total = middle_sum + jnp.sum(jnp.where(inside, edge, 0.0), 0, keepdims=True)
        square = middle_square + jnp.sum(jnp.where(inside, edge_square, 0.0), 0, keepdims=True)
        mean = total / WIN
        means.append(mean)
        scales.append(lax.rsqrt(square / WIN - mean * mean + epsilon))
    return shifted, means, scales


def split(value):
    high = value.astype(jnp.bfloat16)
    return high, (value - high.astype(jnp.float32)).astype(jnp.bfloat16)


def left_kernel(index_ref, span_ref, left_ref):
    offset = index_ref[0]
    shifted, means, scales = window_stats(span_ref[...], offset)
    rows, width = shifted.shape
    filler = jnp.zeros((16 - 2 * ENDS_DEV, width), jnp.float32)
    columns = jnp.concatenate(means + scales + [filler], 0).T
    turned = shifted.T
    day = lax.broadcasted_iota(jnp.int32, (width, rows), 1) - offset
    for end in range(ENDS_DEV):
        mean = columns[:, end : end + 1]
        scale = columns[:, ENDS_DEV + end : ENDS_DEV + end + 1]
        inside = (day >= end) & (day < end + WIN)
        high, low = split(jnp.where(inside, (turned - mean) * (scale / WIN), 0.0))
        left_ref[end, :, 0:rows] = high
        left_ref[end, :, rows : 2 * rows] = high
        left_ref[end, :, 2 * rows : 3 * rows] = low


def left_factors(index, span):
    rows, width = span.shape
    return pl.pallas_call(
        left_kernel,
        out_shape=jax.ShapeDtypeStruct((ENDS_DEV, width, 3 * rows), jnp.bfloat16),
        in_specs=[pl.BlockSpec(memory_space=pltpu.SMEM), pl.BlockSpec(memory_space=pltpu.VMEM)],
        out_specs=pl.BlockSpec(memory_space=pltpu.VMEM),
        compiler_params=pltpu.CompilerParams(vmem_limit_bytes=12 << 20),
        cost_estimate=pl.CostEstimate(flops=6000000000, bytes_accessed=0, transcendentals=0),
        name="left_factors",
    )(index, span)


def tile_kernel(index_ref, left_ref, *refs, blocks):
    spans = refs[:blocks]
    output_ref, tile_ref, sem = refs[-3:]
    width = spans[0].shape[1]
    copies = []
    for block in range(blocks):
        shifted, _, scales = window_stats(spans[block][...], index_ref[0])
        high, low = split(shifted)
        right = jnp.concatenate([high, low, high], 0)
        column = index_ref[1 + block] * width
        for end in range(ENDS_DEV):
            gram = jnp.dot(left_ref[end], right, preferred_element_type=jnp.float32)
            tile_ref[block, end] = (gram * scales[end]).astype(jnp.bfloat16)
            copy = pltpu.make_async_copy(
                tile_ref.at[block, end],
                output_ref.at[end, :, pl.ds(column, width)],
                sem.at[block, end],
            )
            copy.start()
            copies.append(copy)
    for copy in copies:
        copy.wait()


def tiles(index, left, spans, output, output_shape):
    blocks = len(spans)
    ends, height, _ = left.shape
    width = spans[0].shape[1]
    args = [index, left, *spans]
    specs = [pl.BlockSpec(memory_space=pltpu.SMEM)] + [pl.BlockSpec(memory_space=pltpu.VMEM)] * (1 + blocks)
    aliases = {}
    if output is not None:
        aliases = {len(args): 0}
        args.append(output)
        specs.append(pl.BlockSpec(memory_space=pl.ANY))
    return pl.pallas_call(
        lambda *refs: tile_kernel(*refs, blocks=blocks),
        out_shape=jax.ShapeDtypeStruct(output_shape, jnp.bfloat16),
        in_specs=specs,
        out_specs=pl.BlockSpec(memory_space=pl.ANY),
        scratch_shapes=[
            pltpu.VMEM((blocks, ends, height, width), jnp.bfloat16),
            pltpu.SemaphoreType.DMA((blocks, ends)),
        ],
        input_output_aliases=aliases,
        compiler_params=pltpu.CompilerParams(vmem_limit_bytes=20 << 20),
        cost_estimate=pl.CostEstimate(flops=12000000000, bytes_accessed=0, transcendentals=0),
        name="tiles",
    )(*args)


def partner(value, bits):
    pairs = [(source, source ^ bits) for source in range(lax.axis_size("asset"))]
    return lax.ppermute(value, "asset", pairs)


def correlations(day_ranks, confidence):
    days_dev, width = day_ranks.shape
    time_count = lax.axis_size("tm")
    asset_count = lax.axis_size("asset")
    days = days_dev * time_count
    lead_days = days - ENDS_DEV * time_count - WIN + 1
    time_index = lax.axis_index("tm")
    own_index = lax.axis_index("asset")
    first_day = lead_days + time_index * ENDS_DEV
    start = jnp.minimum(first_day, days - ROWS)
    offset = first_day - start

    scores = confidence * (day_ranks - (WIN + 1)).astype(jnp.float32) / WIN
    all_days = jnp.zeros((days, width), jnp.float32)
    for steps in range(time_count):
        shard = scores
        if steps:
            pairs = [(source, source ^ steps) for source in range(time_count)]
            shard = lax.ppermute(scores, "tm", pairs)
        place = (time_index ^ steps) * days_dev
        all_days = lax.dynamic_update_slice_in_dim(all_days, shard, place, 0)
    span = lax.dynamic_slice_in_dim(all_days, start, ROWS, 0)

    hops = range(0, asset_count, 2)
    arrived = {0: span}
    for bits in hops[1:]:
        arrived[bits] = partner(span, bits)
    left = left_factors(jnp.stack([offset]).astype(jnp.int32), span)
    output = None
    for bits in hops:
        pair = [arrived[bits], partner(arrived[bits], 1)]
        index = jnp.stack([offset, own_index ^ bits, own_index ^ bits ^ 1]).astype(jnp.int32)
        output = tiles(index, left, pair, output, (ENDS_DEV, width, width * asset_count))
    return output


def solution(mesh):
    return jax.shard_map(
        correlations,
        mesh=mesh,
        in_specs=(P("tm", "asset"), P("tm", "asset")),
        out_specs=P("tm", "asset", None),
        check_vma=False,
    )
```

time: 150 us -> 51 us (0.34)
  matrix products: 49.6 us -> 0 us
  waiting for transfers between devices: 46.6 us -> 15.7 us
  other arithmetic: 23 us -> 1.17 us
  Pallas kernels: 0 us -> 21.6 us
  blocking collectives: 15.9 us -> 0 us
  local copies, waits for them, and re-layouts: 13.3 us -> 2.38 us
  starting transfers between devices: 0.35 us -> 9.85 us
    dot_general x48 -> x0, matrix products: 49.6 us -> none  [window_gram(): lax.dot_general(left_rows[start_index:stop_index], right_rows[start_index...]
    ppermute x7 -> x10, waiting for transfers between devices: 46.6 us -> 15.7 us  [the longest x7 10.8 us: partner(): return lax.ppermute(value, 'asset', pairs)]
    pallas_call x0 -> x5, Pallas kernels: none -> 21.6 us  [the longest x4 20.4 us: tiles(): pl.pallas_call(lambda *refs: tile_kernel(*refs, blocks=blocks), out_shape...]
    dynamic_update_slice x8 -> x0, other arithmetic: 19.1 us -> none  [the longest x7 17.7 us: rotate_once(): lax.dynamic_update_slice_in_dim(current, cross_tile(own_span, own_moments...]
    all_gather x1 -> x0, blocking collectives: 15.9 us -> none  [per_device(): all_days = lax.all_gather(scores, 'tm', axis=0, tiled=True)]
    ppermute x7 -> x10, starting transfers between devices: 0.35 us -> 9.85 us  [the longest x3 5.71 us: correlations(): shard = lax.ppermute(scores, 'tm', pairs)]
    unnamed x9 -> x0, local copies, waits for them, and re-layouts: 9.12 us -> none
    broadcast_in_dim x1, local copies, waits for them, and re-layouts: 3.06 us -> 0.02 us  [correlations(): all_days = jnp.zeros((days, width), jnp.float32)]
  transfers between devices with their start and end apart: 7 -> 10, of which waited for: 7 -> 3; matrix products, arithmetic and copies ran while one was open for 0% -> 4% of each run, Pallas kernels for 0% -> 32%
where the time goes in v1:
time: 51 us; the launch traced here: 50.9 us
  Pallas kernels  21.6 us (42%)
  waiting for transfers between devices  15.7 us (31%)
  starting transfers between devices  9.85 us (19%)
  local copies, waits for them, and re-layouts  2.38 us (5%)
  other arithmetic  1.17 us (2%)
    pallas_call x4, Pallas kernels, tiles(): pl.pallas_call(lambda *refs: tile_kernel(*refs, blocks=blocks), out_shape...  20.4 us
    ppermute x7, waiting for transfers between devices, partner(): return lax.ppermute(value, 'asset', pairs)  10.8 us
    ppermute x3, starting transfers between devices, correlations(): shard = lax.ppermute(scores, 'tm', pairs)  5.71 us
    ppermute x3, waiting for transfers between devices, correlations(): shard = lax.ppermute(scores, 'tm', pairs)  4.98 us
    ppermute x7, starting transfers between devices, partner(): return lax.ppermute(value, 'asset', pairs)  4.14 us
    dynamic_update_slice x4, local copies, waits for them, and re-layouts, correlations(): all_days = lax.dynamic_update_slice_in_dim(all_days, shard, place, 0)  2.32 us
    pallas_call x1, Pallas kernels, left_factors(): pl.pallas_call(left_kernel, out_shape=jax.ShapeDtypeStruct((ENDS_DEV, wid...  1.22 us
  transfers between devices with their start and end apart: 10, of which 3 were waited for; matrix products, arithmetic and copies ran while one was open for 4% of the time, Pallas kernels for 32%

profile of v1, /device:TPU:0, one launch (start us, length us, event | category | flops | bytes accessed | tf_op | source)
XLA Modules:
  0.0 50.9 jit_solution(16442156321485933042)
XLA Ops:
  0.0 0.9 %multiply_multiply_fusion = f32[36,512]{1,0:T(8,128)S(1)} fusion(f32[36,512]{1,0:T(8,128)} %param.3, s32[36,512]{1,0:T(8,128)} %param.2), kind=kLoop, calls=%fused_computation | loop fusion | flops 73728 | bytes 221184 | tf_op jit(solution)/shard_map/div | solution.py:145
  0.9 3.1 %collective-permute-start = (f32[36,512]{1,0:T(8,128)S(1)}, f32[36,512]{1,0:T(8,128)S(1)}, u32[]{:S(2)}, u32[]{:S(2)}) collective-permute-start(f32[36,512]{1,0:T(8,128)S(1)} %multiply_multiply_fusion), channel_id=1, source_target_pairs={{0,1},{1,0},{2,3},{3,2},{4,5},{5,4},{6,7},{7,6},{8,9},{9,8},{10,11... | collective-permute-start | bytes 221192 | tf_op jit(solution)/shard_map/ppermute | solution.py:151
  4.1 2.6 %collective-permute-start.1 = (f32[36,512]{1,0:T(8,128)S(1)}, f32[36,512]{1,0:T(8,128)S(1)}, u32[]{:S(2)}, u32[]{:S(2)}) collective-permute-start(f32[36,512]{1,0:T(8,128)S(1)} %multiply_multiply_fusion), channel_id=1, source_target_pairs={{0,2},{1,3},{2,0},{3,1},{4,6},{5,7},{6,4},{7,5},{8,10},{9,11},{10,... | collective-permute-start | bytes 221192 | tf_op jit(solution)/shard_map/ppermute | solution.py:151
  6.7 0.0 collective-permute-start.2
  6.7 0.7 %dynamic_update_slice.12 = f32[144,512]{1,0:T(8,128)S(1)} dynamic-update-slice(f32[144,512]{1,0:T(8,128)S(1)} %broadcast_in_dim.3, f32[36,512]{1,0:T(8,128)S(1)} %multiply_multiply_fusion, s32[]{:T(128)S(6)} %select_n.15, s32[]{:T(128)} %constant.30.clone.1) | dynamic-update-slice | bytes 147460 | tf_op jit(solution)/shard_map/dynamic_update_slice | solution.py:153
  7.4 0.1 pad_add_fusion.3.refs_0_
  7.5 0.1 pad_add_fusion
  7.5 0.1 pad_add_fusion.2.refs_0_
  7.6 0.0 collective-permute-done
  7.6 0.6 %dynamic_update_slice.13 = f32[144,512]{1,0:T(8,128)S(1)} dynamic-update-slice(f32[144,512]{1,0:T(8,128)S(1)} %dynamic_update_slice.12, f32[36,512]{1,0:T(8,128)S(1)} %collective-permute-done, s32[]{:T(128)S(6)} %select_n.16, s32[]{:T(128)} %constant.30.clone.1) | dynamic-update-slice | bytes 147460 | tf_op jit(solution)/shard_map/dynamic_update_slice | solution.py:153
  8.3 5.0 %collective-permute-done.1 = f32[36,512]{1,0:T(8,128)S(1)} collective-permute-done((f32[36,512]{1,0:T(8,128)S(1)}, f32[36,512]{1,0:T(8,128)S(1)}, u32[]{:S(2)}, u32[]{:S(2)}) %collective-permute-start.1) | collective-permute-done | bytes 73760 | tf_op jit(solution)/shard_map/ppermute | solution.py:151
  13.3 0.6 %dynamic_update_slice.14 = f32[144,512]{1,0:T(8,128)S(1)} dynamic-update-slice(f32[144,512]{1,0:T(8,128)S(1)} %dynamic_update_slice.13, f32[36,512]{1,0:T(8,128)S(1)} %collective-permute-done.1, s32[]{:T(128)S(6)} %select_n.17, s32[]{:T(128)} %constant.30.clone.1) | dynamic-update-slice | bytes 147460 | tf_op jit(solution)/shard_map/dynamic_update_slice | solution.py:153
  13.8 0.0 collective-permute-done.2
  13.8 0.4 dynamic_update_slice.15
  14.3 0.1 collective-permute-start.9
  14.4 1.6 %collective-permute-start.7 = (f32[128,512]{1,0:T(8,128)S(1)}, f32[128,512]{1,0:T(8,128)S(1)}, u32[]{:S(2)}, u32[]{:S(2)}) collective-permute-start(f32[128,512]{1,0:T(8,128)S(1)} %constant_dynamic-slice_fusion.span_ref.refs_2_), channel_id=1, source_target_pairs={{0,8},{4,12},{8,0},{12,4},{16,24},{20,28},{24,16},{28,20},{1,9},{5... | collective-permute-start | bytes 786440 | tf_op jit(solution)/shard_map/ppermute | solution.py:130
  16.0 1.5 %collective-permute-start.5 = (f32[128,512]{1,0:T(8,128)S(1)}, f32[128,512]{1,0:T(8,128)S(1)}, u32[]{:S(2)}, u32[]{:S(2)}) collective-permute-start(f32[128,512]{1,0:T(8,128)S(1)} %constant_dynamic-slice_fusion.span_ref.refs_2_), channel_id=1, source_target_pairs={{0,16},{4,20},{8,24},{12,28},{16,0},{20,4},{24,8},{28,12},{1,17},{... | collective-permute-start | bytes 786440 | tf_op jit(solution)/shard_map/ppermute | solution.py:130
  17.5 0.5 collective-permute-start.3
  18.0 1.2 %left_factors.1.refs_1_ = bf16[6,512,384]{2,1,0:T(8,128)(2,1)S(1)} custom-call(s32[1]{0:T(128)} %bitcast.index_ref, f32[128,512]{1,0:T(8,128)S(1)} %constant_dynamic-slice_fusion.span_ref.refs_2_), custom_call_target="tpu_custom_call" | custom-call | flops 6000000000 | tf_op jit(solution)/shard_map/left_factors/pallas_call | solution.py:66
  19.2 4.5 %collective-permute-done.7.refs_2_ = f32[128,512]{1,0:T(8,128)S(1)} collective-permute-done((f32[128,512]{1,0:T(8,128)S(1)}, f32[128,512]{1,0:T(8,128)S(1)}, u32[]{:S(2)}, u32[]{:S(2)}) %collective-permute-start.7) | collective-permute-done | bytes 262176 | tf_op jit(solution)/shard_map/ppermute | solution.py:130
  23.6 0.0 collective-permute-start.8
  23.6 6.3 %collective-permute-done.5.refs_2_ = f32[128,512]{1,0:T(8,128)S(1)} collective-permute-done((f32[128,512]{1,0:T(8,128)S(1)}, f32[128,512]{1,0:T(8,128)S(1)}, u32[]{:S(2)}, u32[]{:S(2)}) %collective-permute-start.5) | collective-permute-done | bytes 262176 | tf_op jit(solution)/shard_map/ppermute | solution.py:130
  29.9 0.0 collective-permute-start.6
  29.9 0.0 collective-permute-done.3.refs_2_
  29.9 0.5 collective-permute-start.4
  30.5 0.0 collective-permute-done.9.refs_3_
  30.5 5.1 %tiles.4.refs_4_ = bf16[6,512,4096]{2,1,0:T(8,128)(2,1)} custom-call(s32[3]{0:T(128)S(1)} %pad_add_fusion.3.refs_0_, bf16[6,512,384]{2,1,0:T(8,128)(2,1)S(1)} %left_factors.1.refs_1_, f32[128,512]{1,0:T(8,128)S(1)} %constant_dynamic-slice_fusion.span_ref.refs_2_, f32[128,512]{1,0:T(8,128)S(1)} %collective-permute-done.9.refs_3_), custom_call_target="tpu_custom_call" | custom-call | flops 12000000000 | tf_op jit(solution)/shard_map/tiles/pallas_call | solution.py:112
  35.5 0.0 collective-permute-done.8.refs_3_
  35.6 5.1 %tiles.5.refs_4_ = bf16[6,512,4096]{2,1,0:T(8,128)(2,1)} custom-call(s32[3]{0:T(128)S(1)} %pad_add_fusion.2.refs_0_, bf16[6,512,384]{2,1,0:T(8,128)(2,1)S(1)} %left_factors.1.refs_1_, f32[128,512]{1,0:T(8,128)S(1)} %collective-permute-done.7.refs_2_, f32[128,512]{1,0:T(8,128)S(1)} %collective-permute-done.8.refs_3_, ...), custom_call_target="tpu_custom_call", output_to_operand_aliasing={{}: (4, {})} | custom-call | flops 12000000000 | tf_op jit(solution)/shard_map/tiles/pallas_call | solution.py:112
  40.7 0.0 collective-permute-done.6.refs_3_
  40.7 5.1 %tiles.6.refs_4_ = bf16[6,512,4096]{2,1,0:T(8,128)(2,1)} custom-call(s32[3]{0:T(128)S(1)} %get-tuple-element.6.refs_0_, bf16[6,512,384]{2,1,0:T(8,128)(2,1)S(1)} %left_factors.1.refs_1_, f32[128,512]{1,0:T(8,128)S(1)} %collective-permute-done.5.refs_2_, f32[128,512]{1,0:T(8,128)S(1)} %collective-permute-done.6.refs_3_, ...), custom_call_target="tpu_custom_call", output_to_operand_aliasing={{}: (4, {})} | custom-call | flops 12000000000 | tf_op jit(solution)/shard_map/tiles/pallas_call | solution.py:112
  45.8 0.0 collective-permute-done.4.refs_3_
  45.8 5.1 %tiles.7 = bf16[6,512,4096]{2,1,0:T(8,128)(2,1)} custom-call(s32[3]{0:T(128)S(1)} %get-tuple-element.5.refs_0_, bf16[6,512,384]{2,1,0:T(8,128)(2,1)S(1)} %left_factors.1.refs_1_, f32[128,512]{1,0:T(8,128)S(1)} %collective-permute-done.3.refs_2_, f32[128,512]{1,0:T(8,128)S(1)} %collective-permute-done.4.refs_3_, ...), custom_call_target="tpu_custom_call", output_to_operand_aliasing={{}: (4, {})} | custom-call | flops 12000000000 | tf_op jit(solution)/shard_map/tiles/pallas_call | solution.py:112
  (2 shorter events, 0.1 us)
Async XLA Ops:
  0.9 6.7 %collective-permute-start = (f32[36,512]{1,0:T(8,128)S(1)}, f32[36,512]{1,0:T(8,128)S(1)}, u32[]{:S(2)}, u32[]{:S(2)}) collective-permute-start(f32[36,512]{1,0:T(8,128)S(1)} %multiply_multiply_fusion), channel_id=1, source_target_pairs={{0,1},{1,0},{2,3},{3,2},{4,5},{5,4},{6,7},{7,6},{8,9},{9,8},{10,11... | collective-permute-start | bytes 221192 | tf_op jit(solution)/shard_map/ppermute | solution.py:151
  4.1 9.2 %collective-permute-start.1 = (f32[36,512]{1,0:T(8,128)S(1)}, f32[36,512]{1,0:T(8,128)S(1)}, u32[]{:S(2)}, u32[]{:S(2)}) collective-permute-start(f32[36,512]{1,0:T(8,128)S(1)} %multiply_multiply_fusion), channel_id=1, source_target_pairs={{0,2},{1,3},{2,0},{3,1},{4,6},{5,7},{6,4},{7,5},{8,10},{9,11},{10,... | collective-permute-start | bytes 221192 | tf_op jit(solution)/shard_map/ppermute | solution.py:151
  6.7 7.2 %collective-permute-start.2 = (f32[36,512]{1,0:T(8,128)S(1)}, f32[36,512]{1,0:T(8,128)S(1)}, u32[]{:S(2)}, u32[]{:S(2)}) collective-permute-start(f32[36,512]{1,0:T(8,128)S(1)} %multiply_multiply_fusion), channel_id=1, source_target_pairs={{0,3},{1,2},{2,1},{3,0},{4,7},{5,6},{6,5},{7,4},{8,11},{9,10},{10,... | collective-permute-start | bytes 221192 | tf_op jit(solution)/shard_map/ppermute | solution.py:151
  14.3 16.1 %collective-permute-start.9 = (f32[128,512]{1,0:T(8,128)S(1)}, f32[128,512]{1,0:T(8,128)S(1)}, u32[]{:S(2)}, u32[]{:S(2)}) collective-permute-start(f32[128,512]{1,0:T(8,128)S(1)} %constant_dynamic-slice_fusion.span_ref.refs_2_), channel_id=1, source_target_pairs={{0,4},{4,0},{8,12},{12,8},{16,20},{20,16},{24,28},{28,24},{1,5},{5... | collective-permute-start | bytes 786440 | tf_op jit(solution)/shard_map/ppermute | solution.py:130
  14.4 9.2 %collective-permute-start.7 = (f32[128,512]{1,0:T(8,128)S(1)}, f32[128,512]{1,0:T(8,128)S(1)}, u32[]{:S(2)}, u32[]{:S(2)}) collective-permute-start(f32[128,512]{1,0:T(8,128)S(1)} %constant_dynamic-slice_fusion.span_ref.refs_2_), channel_id=1, source_target_pairs={{0,8},{4,12},{8,0},{12,4},{16,24},{20,28},{24,16},{28,20},{1,9},{5... | collective-permute-start | bytes 786440 | tf_op jit(solution)/shard_map/ppermute | solution.py:130
  16.0 14.0 %collective-permute-start.5 = (f32[128,512]{1,0:T(8,128)S(1)}, f32[128,512]{1,0:T(8,128)S(1)}, u32[]{:S(2)}, u32[]{:S(2)}) collective-permute-start(f32[128,512]{1,0:T(8,128)S(1)} %constant_dynamic-slice_fusion.span_ref.refs_2_), channel_id=1, source_target_pairs={{0,16},{4,20},{8,24},{12,28},{16,0},{20,4},{24,8},{28,12},{1,17},{... | collective-permute-start | bytes 786440 | tf_op jit(solution)/shard_map/ppermute | solution.py:130
  17.5 12.5 %collective-permute-start.3 = (f32[128,512]{1,0:T(8,128)S(1)}, f32[128,512]{1,0:T(8,128)S(1)}, u32[]{:S(2)}, u32[]{:S(2)}) collective-permute-start(f32[128,512]{1,0:T(8,128)S(1)} %constant_dynamic-slice_fusion.span_ref.refs_2_), channel_id=1, source_target_pairs={{0,24},{4,28},{8,16},{12,20},{16,8},{20,12},{24,0},{28,4},{1,25},{... | collective-permute-start | bytes 786440 | tf_op jit(solution)/shard_map/ppermute | solution.py:130
  23.6 11.9 %collective-permute-start.8 = (f32[128,512]{1,0:T(8,128)S(1)}, f32[128,512]{1,0:T(8,128)S(1)}, u32[]{:S(2)}, u32[]{:S(2)}) collective-permute-start(f32[128,512]{1,0:T(8,128)S(1)} %collective-permute-done.7.refs_2_), channel_id=1, source_target_pairs={{0,4},{4,0},{8,12},{12,8},{16,20},{20,16},{24,28},{28,24},{1,5},{5... | collective-permute-start | bytes 786440 | tf_op jit(solution)/shard_map/ppermute | solution.py:130
  29.9 10.7 %collective-permute-start.6 = (f32[128,512]{1,0:T(8,128)S(1)}, f32[128,512]{1,0:T(8,128)S(1)}, u32[]{:S(2)}, u32[]{:S(2)}) collective-permute-start(f32[128,512]{1,0:T(8,128)S(1)} %collective-permute-done.5.refs_2_), channel_id=1, source_target_pairs={{0,4},{4,0},{8,12},{12,8},{16,20},{20,16},{24,28},{28,24},{1,5},{5... | collective-permute-start | bytes 786440 | tf_op jit(solution)/shard_map/ppermute | solution.py:130
  29.9 15.8 %collective-permute-start.4 = (f32[128,512]{1,0:T(8,128)S(1)}, f32[128,512]{1,0:T(8,128)S(1)}, u32[]{:S(2)}, u32[]{:S(2)}) collective-permute-start(f32[128,512]{1,0:T(8,128)S(1)} %collective-permute-done.3.refs_2_), channel_id=1, source_target_pairs={{0,4},{4,0},{8,12},{12,8},{16,20},{20,16},{24,28},{28,24},{1,5},{5... | collective-permute-start | bytes 786440 | tf_op jit(solution)/shard_map/ppermute | solution.py:130
